TPU v7x, 1024 devices: a whole 4x8x16 slice. The times are simulated.
1024 devices in a mesh: layer: 32 (over z_lo, x), shard: 32 (over y, z_hi, core).
Axes of the slice: x: 4, y: 8, z: 16 (z_hi: 2, z_lo: 8; z = z_hi * 8 + z_lo), core: 2. Of those that a mesh axis runs over, the one named last changes fastest.
Arguments:
- gate_grad: bfloat16 [256, 2048, 512], P('layer', 'shard'), parts along dimension 0, may hold values from -400 to 400
- gate_moment: bfloat16 [256, 2048, 512], P('layer', 'shard'), parts along dimension 0, may hold values from -120 to 120
- down_grad: bfloat16 [256, 2048, 512], P('layer', 'shard'), parts along dimension 0, may hold values from -400 to 400
- down_moment: bfloat16 [256, 2048, 512], P('layer', 'shard'), parts along dimension 0, may hold values from -120 to 120
Outputs:
- gate_update: bfloat16 [256, 2048, 512], P('layer', 'shard'), parts along dimension 0
- down_update: bfloat16 [256, 2048, 512], P('layer', 'shard'), parts along dimension 0
There are 32 independent parts, one for each index of `layer`. A program takes and returns all parts, laid end to end along the dimension named above; each array names one. Nothing has to cross between parts.
All inputs are finite; a program needn't handle non-finite values.
Results may differ from a plain program's by a relative error of at most 0.0068.
Values may be sent and summed in bfloat16 or wider, within the bound.
No kernel may reach another device: no remote copies, remote signals or barrier semaphores. Data moves between devices by JAX's collectives and lax.ppermute only.
A program may use at most 32 MiB of HBM per device.

v0:
```python
import math

import jax
import jax.numpy as jnp
from jax import lax
from jax.sharding import Mesh
from jax.sharding import PartitionSpec as P

D = 2048
SHARD = ("shard_0", "shard_1", "shard_2")


MOMENTUM_RATE = 0.95
COEF_A = 3.4445
COEF_B = -4.775
COEF_C = 2.0315
EPSILON = 1e-07


def partner(block, axis, stride):
    count = lax.axis_size(axis)
    route = []
    for low in range(count):
        high = low | 1 << stride
        if high != low and high < count:
            route += [(low, high), (high, low)]
    return lax.ppermute(block, axis, route)


def in_blocks(shard, dim, peers):
    before, after = (shard.shape[:dim], shard.shape[dim + 1 :])
    return jnp.moveaxis(shard.reshape(*before, peers, -1, *after), dim, 0)


def in_order(parts, dim):
    shape = list(parts.shape[1:])
    shape[dim] *= parts.shape[0]
    return jnp.moveaxis(parts, 0, dim).reshape(shape)


def moved_by_axis(parts, axes, turns):
    shape = [lax.axis_size(a) for a in axes]
    parts = parts.reshape(*shape, *parts.shape[1:])
    for k in turns:
        parts = lax.all_to_all(parts, axes[k], split_axis=k, concat_axis=k, tiled=True)
    return parts.reshape(-1, *parts.shape[len(axes) :])


def two_step_exchange(shard, groups, turns, split_dim, concat_dim):
    peers = lax.axis_size(groups[0]) * lax.axis_size(groups[1])
    parts = in_blocks(shard, split_dim, peers)
    return in_order(moved_by_axis(parts, groups, turns), concat_dim)


def blended(gradient, moment):
    buffer = MOMENTUM_RATE * moment.astype(jnp.float32) + gradient.astype(jnp.float32)
    return (gradient.astype(jnp.float32) + MOMENTUM_RATE * buffer).astype(jnp.bfloat16)


def transposed_product(first_matrix, second_matrix):
    return lax.dot_general(
        first_matrix, second_matrix, (((0,), (0,)), ((), ())), preferred_element_type=jnp.float32
    )


def quintic(current):
    square = jnp.dot(current, current, preferred_element_type=jnp.float32)
    identity = jnp.eye(current.shape[0], dtype=jnp.float32)
    return (COEF_A * identity + COEF_B * current.astype(jnp.float32) + COEF_C * square).astype(
        jnp.bfloat16
    )


def bit_value(position):
    return lax.axis_index(SHARD) // (1 << position) % 2


def ordered_total(ordered):
    total = ordered[0].astype(jnp.float32)
    for member in ordered[1:]:
        total = total + member.astype(jnp.float32)
    return total


def polish(owned_rows, total):
    factor = 1.0 / (jnp.sqrt(jnp.trace(total)) + EPSILON)
    scaled = (total * (factor * factor)).astype(jnp.bfloat16)
    combined = quintic(scaled)
    product = jnp.dot(scaled, combined, preferred_element_type=jnp.float32).astype(jnp.bfloat16)
    current = transposed_product(combined, product).astype(jnp.bfloat16)
    combined = jnp.dot(combined, quintic(current), preferred_element_type=jnp.float32).astype(
        jnp.bfloat16
    )
    result = jnp.dot(owned_rows, combined, preferred_element_type=jnp.float32) * (
        math.sqrt(D) * factor
    )
    return result.astype(jnp.bfloat16)


def paired_owners(gate_input, down_input, pair_bit):
    experts, row_count, columns = gate_input.shape
    matrices = 2 * experts
    group = 1 << pair_bit
    stacked = jnp.concatenate((gate_input, down_input), 0)
    outgoing = stacked.reshape(matrices // group, group, 2, row_count // 2, columns)
    outgoing = outgoing.transpose(0, 2, 1, 3, 4).reshape(matrices * 2, row_count // 2, columns)
    owned_rows = lax.all_to_all(outgoing, SHARD, split_axis=0, concat_axis=1, tiled=True)[0]
    pieces = owned_rows.reshape(-1, 2, row_count // 4, columns)
    lower_rows = pieces[:, 0].reshape(-1, columns)
    upper_rows = pieces[:, 1].reshape(-1, columns)
    own_lower, own_upper = lax.optimization_barrier(
        (
            transposed_product(lower_rows, lower_rows).astype(jnp.bfloat16),
            transposed_product(upper_rows, upper_rows).astype(jnp.bfloat16),
        )
    )
    far_lower, far_upper = partner((own_lower, own_upper), SHARD, pair_bit)
    high = bit_value(pair_bit) == 1
    ordered = (
        jnp.where(high, far_lower, own_lower),
        jnp.where(high, far_upper, own_upper),
        jnp.where(high, own_lower, far_lower),
        jnp.where(high, own_upper, far_upper),
    )
    result = polish(owned_rows, ordered_total(ordered))
    returned = two_step_exchange(result[None], (("shard_0", "shard_1"), "shard_2"), (0, 1), 1, 0)
    restored = returned.reshape(matrices // group, 2, group, row_count // 2, columns)
    restored = restored.transpose(0, 2, 1, 3, 4).reshape(matrices, row_count, columns)
    return (restored[:experts], restored[experts:])


def shards(gate_grad, gate_moment, down_grad, down_moment):
    first_bit = 0
    gate_input = blended(gate_grad, gate_moment)
    down_input = blended(down_grad, down_moment)
    gate_update, down_update = paired_owners(gate_input, down_input, first_bit)
    return (gate_update, down_update)


def solution(mesh):
    split = Mesh(
        mesh.devices.reshape(mesh.shape["layer"], 8, 2, 2),
        ("layer", "shard_0", "shard_1", "shard_2"),
    )
    in_specs = (
        P("layer", SHARD, None),
        P("layer", SHARD, None),
        P("layer", SHARD, None),
        P("layer", SHARD, None),
    )
    out_specs = (P("layer", SHARD, None), P("layer", SHARD, None))
    return jax.shard_map(
        shards, mesh=split, in_specs=in_specs, out_specs=out_specs, check_vma=False
    )
```

profile of v0, /device:TPU:83, one launch (start us, length us, event | category | flops | bytes accessed | tf_op | source)
XLA Modules:
  0.0 164.4 jit_solution(4715253663101479997)
XLA Ops:
  0.6 2.0 %fusion.7 = (bf16[8,64,512]{2,1,0:T(8,128)(2,1)S(1)}, bf16[8,64,512]{2,1,0:T(8,128)(2,1)S(1)}) fusion(bf16[8,64,512]{2,1,0:T(8,128)(2,1)} %param.4, bf16[8,64,512]{2,1,0:T(8,128)(2,1)} %param.5, bf16[8,64,512]{2,1,0:T(8,128)(2,1)} %param.7, bf16[8,64,512]{2,1,0:T(8,128)(2,1)} %param.6), kind=kLoop, calls=%fused_computation.21 | loop fusion | flops 3670016 | bytes 3145728 | tf_op jit(solution)/shard_map/convert_element_type | solution.py:57
  2.6 0.1 pad_maximum_fusion
  2.7 80.7 %all_to_all.19 = bf16[32,32,512]{2,1,0:T(8,128)(2,1)S(1)} all-to-all(bf16[32,32,512]{2,1,0:T(8,128)(2,1)S(1)} %bitcast.30), channel_id=1, replica_groups=mesh['layer'=32,'shard_0'=8,'shard_1'=2,'shard_2'=2] {'shard_0','shard_1..., dimensions={0} | all-to-all | bytes 2097152 | tf_op jit(solution)/shard_map/all_to_all | solution.py:107
  83.4 0.6 copy.11
  83.9 0.5 fusion.5
  84.4 0.5 fusion.4
  84.9 3.9 %collective-permute-start = (bf16[512,512]{1,0:T(8,128)(2,1)S(1)}, bf16[512,512]{1,0:T(8,128)(2,1)S(1)}, u32[]{:S(2)}, u32[]{:S(2)}) collective-permute-start(bf16[512,512]{1,0:T(8,128)(2,1)S(1)} %fusion.4), channel_id=1, source_target_pairs={{0,1},{1,0},{2,3},{3,2},{4,5},{5,4},{6,7},{7,6},{8,9},{9,8},{10,11... | collective-permute-start | bytes 1572872 | tf_op jit(solution)/shard_map/ppermute | solution.py:27
  88.8 1.9 %collective-permute-start.1 = (bf16[512,512]{1,0:T(8,128)(2,1)S(1)}, bf16[512,512]{1,0:T(8,128)(2,1)}, u32[]{:S(2)}, u32[]{:S(2)}) collective-permute-start(bf16[512,512]{1,0:T(8,128)(2,1)S(1)} %fusion.5), channel_id=1, source_target_pairs={{0,1},{1,0},{2,3},{3,2},{4,5},{5,4},{6,7},{7,6},{8,9},{9,8},{10,11... | collective-permute-start | bytes 1572872 | tf_op jit(solution)/shard_map/ppermute | solution.py:27
  90.7 0.0 collective-permute-done
  90.7 0.0 copy-start
  90.7 0.8 copy-done
  91.5 1.2 collective-permute-done.1
  92.7 2.2 %select_reduce_fusion = (f32[]{:T(128)}, f32[512,512]{1,0:T(8,128)S(1)}) fusion(bf16[512,512]{1,0:T(8,128)(2,1)S(1)} %fusion.5, bf16[512,512]{1,0:T(8,128)(2,1)} %collective-permute-done.1, bf16[512,512]{1,0:T(8,128)(2,1)S(1)} %fusion.4, bf16[512,512]{1,0:T(8,128)(2,1)} %copy-done, pred[]{:T(512)S(6)} %eq.16), kind=kLoop, calls=%fused_computation.28 | loop fusion | flops 3670015 | bytes 3145733 | tf_op jit(solution)/shard_map/jit(trace)/reduce_sum | solution.py:86
  95.6 0.5 fusion.2
  96.1 0.8 convolution_convert_fusion.1
  96.9 0.8 convolution_convert_fusion
  97.7 0.7 multiply_convert_fusion
  98.4 59.1 %all_to_all.20 = bf16[16,2,1,32,512]{4,3,1,2,0:T(8,128)(2,1)S(1)} all-to-all(bf16[16,2,1,32,512]{4,3,1,2,0:T(8,128)(2,1)S(1)} %bitcast.31), channel_id=1, replica_groups=mesh['layer'=32,'shard_0'=8,'shard_1'=2,'shard_2'=2] {'shard_0','shard_1'}, dimensions={0} | all-to-all | bytes 2097152 | tf_op jit(solution)/shard_map/all_to_all | solution.py:45
  157.5 0.1 copy.13
  157.6 5.0 %all_to_all.21 = bf16[16,2,1,32,512]{4,3,0,2,1:T(8,128)(2,1)S(1)} all-to-all(bf16[16,2,1,32,512]{4,3,0,2,1:T(8,128)(2,1)S(1)} %copy.13), channel_id=1, replica_groups=mesh['layer'=32,'shard_0'=8,'shard_1'=2,'shard_2'=2] {'shard_2'}, dimensions={1} | all-to-all | bytes 2097152 | tf_op jit(solution)/shard_map/all_to_all | solution.py:45
  162.6 0.1 fusion.20
  162.7 0.8 copy.17
  163.5 0.8 copy.16
Async XLA Ops:
  84.9 5.8 %collective-permute-start = (bf16[512,512]{1,0:T(8,128)(2,1)S(1)}, bf16[512,512]{1,0:T(8,128)(2,1)S(1)}, u32[]{:S(2)}, u32[]{:S(2)}) collective-permute-start(bf16[512,512]{1,0:T(8,128)(2,1)S(1)} %fusion.4), channel_id=1, source_target_pairs={{0,1},{1,0},{2,3},{3,2},{4,5},{5,4},{6,7},{7,6},{8,9},{9,8},{10,11... | collective-permute-start | bytes 1572872 | tf_op jit(solution)/shard_map/ppermute | solution.py:27
  88.8 3.9 %collective-permute-start.1 = (bf16[512,512]{1,0:T(8,128)(2,1)S(1)}, bf16[512,512]{1,0:T(8,128)(2,1)}, u32[]{:S(2)}, u32[]{:S(2)}) collective-permute-start(bf16[512,512]{1,0:T(8,128)(2,1)S(1)} %fusion.5), channel_id=1, source_target_pairs={{0,1},{1,0},{2,3},{3,2},{4,5},{5,4},{6,7},{7,6},{8,9},{9,8},{10,11... | collective-permute-start | bytes 1572872 | tf_op jit(solution)/shard_map/ppermute | solution.py:27
  90.7 0.8 copy-start
where the time goes:
time: 165 us; the launch traced here: 164 us
  blocking collectives  145 us (88%)
  starting transfers between devices  5.78 us (4%)
  other arithmetic  4.27 us (3%)
  matrix products  3.68 us (2%)
  local copies, waits for them, and re-layouts  3.19 us (2%)
    all_to_all x1, blocking collectives, paired_owners(): lax.all_to_all(outgoing, SHARD, split_axis=0, concat_axis=1, tiled=True)[0]  80.7 us
    all_to_all x2, blocking collectives, moved_by_axis(): lax.all_to_all(parts, axes[k], split_axis=k, concat_axis=k, tiled=True)  64.1 us
    ppermute x2, starting transfers between devices, partner(): return lax.ppermute(block, axis, route)  5.78 us
  transfers between devices with their start and end apart: 2, of which 1 were waited for; matrix products, arithmetic and copies ran while one was open for 0% of the time, Pallas kernels for 0%

commit v1 on v0

v1 whole, which is shorter than its diff:
```python
import math

import jax
import jax.numpy as jnp
from jax import lax
from jax.sharding import Mesh
from jax.sharding import PartitionSpec as P

D = 2048
SHARD = ("y", "z_hi", "core")
HALF = ("y", "core")

MOMENTUM_RATE = 0.95
COEF_A = 3.4445
COEF_B = -4.775
COEF_C = 2.0315
EPSILON = 1e-07


def blended(gradient, moment):
    buffer = MOMENTUM_RATE * moment.astype(jnp.float32) + gradient.astype(jnp.float32)
    return (gradient.astype(jnp.float32) + MOMENTUM_RATE * buffer).astype(jnp.bfloat16)


def transposed_product(first_matrix, second_matrix):
    return lax.dot_general(
        first_matrix, second_matrix, (((0,), (0,)), ((), ())), preferred_element_type=jnp.float32
    )


def quintic(current):
    square = jnp.dot(current, current, preferred_element_type=jnp.float32)
    identity = jnp.eye(current.shape[0], dtype=jnp.float32)
    return (COEF_A * identity + COEF_B * current.astype(jnp.float32) + COEF_C * square).astype(
        jnp.bfloat16
    )


def positions(size):
    shape = (size, size)
    return lax.broadcasted_iota(jnp.int32, shape, 0), lax.broadcasted_iota(jnp.int32, shape, 1)


def pack(gram):
    half = gram.shape[0] // 2
    row, column = positions(half)
    first, second = gram[:half, :half], gram[half:, half:]
    diagonal = jnp.sum(jnp.where(row == column, first, 0.0), 0)
    return jnp.concatenate(
        (
            gram[:half, half:],
            jnp.where(row < column, first, second),
            jnp.broadcast_to(diagonal, (8, half)),
        ),
        0,
    )


def unpack(packed):
    half = packed.shape[1]
    row, column = positions(half)
    corner, both, diagonal = packed[:half], packed[half : 2 * half], packed[2 * half]
    mirrored = both.T
    first = jnp.where(row < column, both, jnp.where(row == column, diagonal, mirrored))
    second = jnp.where(row < column, mirrored, both)
    total = jnp.concatenate(
        (jnp.concatenate((first, corner), 1), jnp.concatenate((corner.T, second), 1)), 0
    )
    trace = jnp.sum(diagonal) + jnp.sum(jnp.where(row == column, both, 0.0))
    return total, trace


def polish(owned_rows, packed_total):
    total, trace = unpack(packed_total)
    factor = 1.0 / (jnp.sqrt(trace) + EPSILON)
    scaled = (total * (factor * factor)).astype(jnp.bfloat16)
    combined = quintic(scaled)
    product = jnp.dot(scaled, combined, preferred_element_type=jnp.float32).astype(jnp.bfloat16)
    current = transposed_product(combined, product).astype(jnp.bfloat16)
    combined = jnp.dot(combined, quintic(current), preferred_element_type=jnp.float32).astype(
        jnp.bfloat16
    )
    result = jnp.dot(owned_rows, combined, preferred_element_type=jnp.float32) * (
        math.sqrt(D) * factor
    )
    return result.astype(jnp.bfloat16)


def exchange(blocks):
    return lax.all_to_all(blocks, HALF, split_axis=0, concat_axis=0, tiled=True)


def shards(gate_grad, gate_moment, down_grad, down_moment):
    experts, row_count, columns = gate_grad.shape
    stacked = jnp.concatenate(
        (blended(gate_grad, gate_moment), blended(down_grad, down_moment)), 0
    )
    owned_rows = exchange(stacked).reshape(-1, columns)
    own = pack(transposed_product(owned_rows, owned_rows)).astype(jnp.bfloat16)
    own = lax.optimization_barrier(own)
    far = lax.ppermute(own, "z_hi", [(0, 1), (1, 0)])
    result = polish(owned_rows, own.astype(jnp.float32) + far.astype(jnp.float32))
    restored = exchange(result.reshape(2 * experts, row_count, columns))
    return restored[:experts], restored[experts:]


def solution(mesh):
    split = Mesh(
        mesh.devices.reshape(mesh.shape["layer"], -1, 2, 2), ("layer", "y", "z_hi", "core")
    )
    spec = P("layer", SHARD, None)
    return jax.shard_map(
        shards, mesh=split, in_specs=(spec,) * 4, out_specs=(spec, spec), check_vma=False
    )
```

time: 165 us -> 122 us (0.74)
  the two profiles are of different devices: /device:TPU:83 before, /device:TPU:65 now
where the time goes in v1:
time: 122 us; the launch traced here: 121 us
  waiting for transfers between devices  50.6 us (41%)
  blocking collectives  32.9 us (27%)
  starting transfers between devices  26 us (21%)
  other arithmetic  4.56 us (4%)
  matrix products  3.63 us (3%)
  between operations  2.13 us (2%)
  local copies, waits for them, and re-layouts  1.7 us (1%)
    all_to_all x1, blocking collectives, exchange(): return lax.all_to_all(blocks, HALF, split_axis=0, concat_axis=0, tiled=True)  32.9 us
    all_to_all x1, waiting for transfers between devices, exchange(): return lax.all_to_all(blocks, HALF, split_axis=0, concat_axis=0, tiled=True)  27.8 us
    ppermute x1, waiting for transfers between devices, shards(): far = lax.ppermute(own, 'z_hi', [(0, 1), (1, 0)])  22.8 us
    ppermute x1, starting transfers between devices, shards(): far = lax.ppermute(own, 'z_hi', [(0, 1), (1, 0)])  18.2 us
    all_to_all x1, starting transfers between devices, exchange(): return lax.all_to_all(blocks, HALF, split_axis=0, concat_axis=0, tiled=True)  7.79 us
  transfers between devices with their start and end apart: 2, of which 2 were waited for; matrix products, arithmetic and copies ran while one was open for 0% of the time, Pallas kernels for 0%

profile of v1, /device:TPU:65, one launch (start us, length us, event | category | flops | bytes accessed | tf_op | source)
XLA Modules:
  0.0 121.4 jit_solution(5905236778039033653)
XLA Ops:
  0.6 2.0 %fusion.5 = (bf16[8,64,512]{2,1,0:T(8,128)(2,1)S(1)}, bf16[8,64,512]{2,1,0:T(8,128)(2,1)S(1)}) fusion(bf16[8,64,512]{2,1,0:T(8,128)(2,1)} %param.4, bf16[8,64,512]{2,1,0:T(8,128)(2,1)} %param.5, bf16[8,64,512]{2,1,0:T(8,128)(2,1)} %param.7, bf16[8,64,512]{2,1,0:T(8,128)(2,1)} %param.6), kind=kLoop, calls=%fused_computation.18 | loop fusion | flops 3670016 | bytes 3145728 | tf_op jit(solution)/shard_map/convert_element_type | solution.py:22
  2.6 1.1 pad_maximum_fusion
  3.7 7.8 %all-to-all-start = ((bf16[16,64,512]{2,1,0:T(8,128)(2,1)}), bf16[16,64,512]{2,1,0:T(8,128)(2,1)S(1)}, u32[]{:S(2)}, u32[]{:S(2)}) async-start(bf16[16,64,512]{2,1,0:T(8,128)(2,1)} %pad_maximum_fusion), calls=%async_computation | async-start | bytes 2097152 | tf_op jit(solution)/shard_map/all_to_all | solution.py:90
  11.5 0.2 copy.7
  11.7 27.8 %all-to-all-done = bf16[16,64,512]{2,1,0:T(8,128)(2,1)S(1)} async-done(((bf16[16,64,512]{2,1,0:T(8,128)(2,1)}), bf16[16,64,512]{2,1,0:T(8,128)(2,1)S(1)}, u32[]{:S(2)}, u32[]{:S(2)}) %all-to-all-start) | async-done | bytes 1048608 | tf_op jit(solution)/shard_map/all_to_all | solution.py:90
  39.5 0.7 convolution_bitcast_fusion
  40.3 0.1 copy.16
  40.4 0.1 select_reduce_fusion.1
  40.6 18.2 %collective-permute-start = (bf16[520,256]{1,0:T(8,128)(2,1)S(1)}, bf16[520,256]{1,0:T(8,128)(2,1)S(1)}, u32[]{:S(2)}, u32[]{:S(2)}) collective-permute-start(bf16[520,256]{1,0:T(8,128)(2,1)S(1)} %pad_maximum_fusion.1), channel_id=1, source_target_pairs={{0,2},{2,0},{1,3},{3,1},{4,6},{6,4},{5,7},{7,5},{8,10},{10,8},{9,1... | collective-permute-start | bytes 798728 | tf_op jit(solution)/shard_map/ppermute | solution.py:101
  58.8 22.8 %collective-permute-done = bf16[520,256]{1,0:T(8,128)(2,1)S(1)} collective-permute-done((bf16[520,256]{1,0:T(8,128)(2,1)S(1)}, bf16[520,256]{1,0:T(8,128)(2,1)S(1)}, u32[]{:S(2)}, u32[]{:S(2)}) %collective-permute-start) | collective-permute-done | bytes 266272 | tf_op jit(solution)/shard_map/ppermute | solution.py:101
  81.5 0.1 convert_add_fusion.4
  81.6 0.6 fusion.26
  82.2 0.1 fusion.27
  82.3 0.1 copy.11
  82.4 0.1 copy.17
  82.5 0.6 fusion.16
  84.6 0.5 fusion.2
  85.0 0.8 convolution_convert_fusion.1
  85.9 0.9 convolution_convert_fusion
  86.8 0.7 multiply_convert_fusion
  87.5 32.9 %all_to_all.10 = bf16[16,64,512]{2,1,0:T(8,128)(2,1)S(1)} all-to-all(bf16[16,64,512]{2,1,0:T(8,128)(2,1)S(1)} %bitcast.22), channel_id=1, replica_groups=mesh['layer'=32,'y'=8,'z_hi'=2,'core'=2] {'y','core'}, dimensions={0} | all-to-all | bytes 2097152 | tf_op jit(solution)/shard_map/all_to_all | solution.py:90
  120.3 1.1 fusion.24
  (5 shorter events, 0.1 us)
Async XLA Ops:
  3.7 35.8 %all-to-all-start = ((bf16[16,64,512]{2,1,0:T(8,128)(2,1)}), bf16[16,64,512]{2,1,0:T(8,128)(2,1)S(1)}, u32[]{:S(2)}, u32[]{:S(2)}) async-start(bf16[16,64,512]{2,1,0:T(8,128)(2,1)} %pad_maximum_fusion), calls=%async_computation | async-start | bytes 2097152 | tf_op jit(solution)/shard_map/all_to_all | solution.py:90
  40.6 41.0 %collective-permute-start = (bf16[520,256]{1,0:T(8,128)(2,1)S(1)}, bf16[520,256]{1,0:T(8,128)(2,1)S(1)}, u32[]{:S(2)}, u32[]{:S(2)}) collective-permute-start(bf16[520,256]{1,0:T(8,128)(2,1)S(1)} %pad_maximum_fusion.1), channel_id=1, source_target_pairs={{0,2},{2,0},{1,3},{3,1},{4,6},{6,4},{5,7},{7,5},{8,10},{10,8},{9,1... | collective-permute-start | bytes 798728 | tf_op jit(solution)/shard_map/ppermute | solution.py:101

commit v2 on v1

v2 whole, which is shorter than its diff:
```python
import math

import jax
import jax.numpy as jnp
from jax import lax
from jax.experimental import pallas as pl
from jax.experimental.pallas import tpu as pltpu
from jax.sharding import Mesh
from jax.sharding import PartitionSpec as P

D = 2048
SHARD = ("y", "z_hi", "core")
HALF = ("y", "core")
GRANT = 16 << 20

MOMENTUM_RATE = 0.95
COEF_A = 3.4445
COEF_B = -4.775
COEF_C = 2.0315
EPSILON = 1e-07

IN_VMEM = pl.BlockSpec(memory_space=pltpu.VMEM)


def blended(gradient, moment):
    buffer = MOMENTUM_RATE * moment.astype(jnp.float32) + gradient.astype(jnp.float32)
    return (gradient.astype(jnp.float32) + MOMENTUM_RATE * buffer).astype(jnp.bfloat16)


def blend_all(gate_grad, gate_moment, down_grad, down_moment):
    return blended(
        jnp.concatenate((gate_grad, down_grad), 0), jnp.concatenate((gate_moment, down_moment), 0)
    )


def positions(size):
    shape = (size, size)
    return lax.broadcasted_iota(jnp.int32, shape, 0), lax.broadcasted_iota(jnp.int32, shape, 1)


def transposed_product(first_matrix, second_matrix):
    return lax.dot_general(
        first_matrix, second_matrix, (((0,), (0,)), ((), ())), preferred_element_type=jnp.float32
    )


def gram_kernel(rows, packed):
    half = rows.shape[1] // 2
    row, column = positions(half)
    packed[:half] = transposed_product(rows[:, :half], rows[:, half:]).astype(jnp.bfloat16)
    first = transposed_product(rows[:, :half], rows[:, :half])
    second = transposed_product(rows[:, half:], rows[:, half:])
    packed[half : 2 * half] = jnp.where(row < column, first, second).astype(jnp.bfloat16)
    diagonal = jnp.sum(jnp.where(row == column, first, 0.0), 0, keepdims=True)
    packed[2 * half :] = jnp.broadcast_to(diagonal, (8, half)).astype(jnp.bfloat16)


def gram(rows):
    half = rows.shape[1] // 2
    return pl.pallas_call(
        gram_kernel,
        out_shape=jax.ShapeDtypeStruct((2 * half + 8, half), jnp.bfloat16),
        in_specs=[IN_VMEM],
        out_specs=IN_VMEM,
        compiler_params=pltpu.CompilerParams(vmem_limit_bytes=GRANT),
        name="gram",
    )(rows)


def product(left, right):
    return jnp.dot(left, right, preferred_element_type=jnp.float32)


def quintic(current):
    row, column = positions(current.shape[0])
    linear = COEF_B * current.astype(jnp.float32) + jnp.where(row == column, COEF_A, 0.0)
    return (linear + COEF_C * product(current, current)).astype(jnp.bfloat16)


def polish_kernel(rows, own, far, out, scaled):
    half = own.shape[1]
    row, column = positions(half)
    packed = own[...].astype(jnp.float32) + far[...].astype(jnp.float32)
    corner, both, diagonal = packed[:half], packed[half : 2 * half], packed[2 * half : 2 * half + 1]
    mirrored = both.T
    first = jnp.where(row < column, both, jnp.where(row == column, diagonal, mirrored))
    second = jnp.where(row < column, mirrored, both)
    on_diagonal = jnp.where(row == column, both, 0.0)
    trace = jnp.sum(
        diagonal + jnp.sum(on_diagonal, 0, keepdims=True), 1, keepdims=True
    )
    factor = 1.0 / (jnp.sqrt(trace) + EPSILON)
    square = factor * factor
    scaled[:half, :half] = (first * square).astype(jnp.bfloat16)
    scaled[half:, half:] = (second * square).astype(jnp.bfloat16)
    corner = corner * square
    scaled[:half, half:] = corner.astype(jnp.bfloat16)
    scaled[half:, :half] = corner.T.astype(jnp.bfloat16)
    current = scaled[...]
    combined = quintic(current)
    current = product(combined, product(current, combined).astype(jnp.bfloat16))
    combined = product(combined, quintic(current.astype(jnp.bfloat16))).astype(jnp.bfloat16)
    out[...] = (product(rows[...], combined) * (math.sqrt(D) * factor)).astype(jnp.bfloat16)


def polish(rows, own, far):
    columns = rows.shape[1]
    return pl.pallas_call(
        polish_kernel,
        out_shape=jax.ShapeDtypeStruct(rows.shape, jnp.bfloat16),
        in_specs=[IN_VMEM] * 3,
        out_specs=IN_VMEM,
        scratch_shapes=[pltpu.VMEM((columns, columns), jnp.bfloat16)],
        compiler_params=pltpu.CompilerParams(vmem_limit_bytes=GRANT),
        name="polish",
    )(rows, own, far)


def exchange(blocks):
    return lax.all_to_all(blocks, HALF, split_axis=0, concat_axis=0, tiled=True)


def shards(gate_grad, gate_moment, down_grad, down_moment):
    experts, row_count, columns = gate_grad.shape
    stacked = blend_all(gate_grad, gate_moment, down_grad, down_moment)
    owned_rows = exchange(stacked).reshape(-1, columns)
    own = gram(owned_rows)
    far = lax.ppermute(own, "z_hi", [(0, 1), (1, 0)])
    result = polish(owned_rows, own, far)
    restored = exchange(result.reshape(2 * experts, row_count, columns))
    return restored[:experts], restored[experts:]


def solution(mesh):
    split = Mesh(
        mesh.devices.reshape(mesh.shape["layer"], -1, 2, 2), ("layer", "y", "z_hi", "core")
    )
    spec = P("layer", SHARD, None)
    return jax.shard_map(
        shards, mesh=split, in_specs=(spec,) * 4, out_specs=(spec, spec), check_vma=False
    )
```

time: 122 us -> 117 us (0.959)
  the two profiles are of different devices: /device:TPU:65 before, /device:TPU:71 now
where the time goes in v2:
time: 117 us; the launch traced here: 116 us
  blocking collectives  68.2 us (58%)
  waiting for transfers between devices  23 us (20%)
  starting transfers between devices  18.2 us (16%)
  Pallas kernels  3.22 us (3%)
  other arithmetic  1.96 us (2%)
    all_to_all x2, blocking collectives, exchange(): return lax.all_to_all(blocks, HALF, split_axis=0, concat_axis=0, tiled=True)  68.2 us
    ppermute x1, waiting for transfers between devices, shards(): far = lax.ppermute(own, 'z_hi', [(0, 1), (1, 0)])  23 us
    ppermute x1, starting transfers between devices, shards(): far = lax.ppermute(own, 'z_hi', [(0, 1), (1, 0)])  18.2 us
    pallas_call x1, Pallas kernels, polish(): pl.pallas_call(polish_kernel, out_shape=jax.ShapeDtypeStruct(rows.shape,...  2.61 us
  transfers between devices with their start and end apart: 1, of which 1 were waited for; matrix products, arithmetic and copies ran while one was open for 0% of the time, Pallas kernels for 0%

profile of v2, /device:TPU:71, one launch (start us, length us, event | category | flops | bytes accessed | tf_op | source)
XLA Modules:
  0.0 116.3 jit_solution(9109530695720516030)
XLA Ops:
  0.6 2.0 %fusion.1 = bf16[16,64,512]{2,1,0:T(8,128)(2,1)S(1)} fusion(bf16[8,64,512]{2,1,0:T(8,128)(2,1)} %param.6, bf16[8,64,512]{2,1,0:T(8,128)(2,1)} %param.4, bf16[8,64,512]{2,1,0:T(8,128)(2,1)} %param.7, bf16[8,64,512]{2,1,0:T(8,128)(2,1)} %param.5), kind=kLoop, calls=%fused_computation.3 | loop fusion | flops 4718592 | bytes 3145728 | tf_op jit(solution)/shard_map/convert_element_type | solution.py:27
  2.6 36.0 %all_to_all.10 = bf16[16,64,512]{2,1,0:T(8,128)(2,1)S(1)} all-to-all(bf16[16,64,512]{2,1,0:T(8,128)(2,1)S(1)} %fusion.1), channel_id=1, replica_groups=mesh['layer'=32,'y'=8,'z_hi'=2,'core'=2] {'y','core'}, dimensions={0} | all-to-all | bytes 2097152 | tf_op jit(solution)/shard_map/all_to_all | solution.py:120
  38.6 0.6 gram.1.own
  39.2 18.2 %collective-permute-start = (bf16[520,256]{1,0:T(8,128)(2,1)S(1)}, bf16[520,256]{1,0:T(8,128)(2,1)S(1)}, u32[]{:S(2)}, u32[]{:S(2)}) collective-permute-start(bf16[520,256]{1,0:T(8,128)(2,1)S(1)} %gram.1.own), channel_id=1, source_target_pairs={{0,2},{2,0},{1,3},{3,1},{4,6},{6,4},{5,7},{7,5},{8,10},{10,8},{9,1... | collective-permute-start | bytes 798728 | tf_op jit(solution)/shard_map/ppermute | solution.py:128
  57.4 23.0 %collective-permute-done.far = bf16[520,256]{1,0:T(8,128)(2,1)S(1)} collective-permute-done((bf16[520,256]{1,0:T(8,128)(2,1)S(1)}, bf16[520,256]{1,0:T(8,128)(2,1)S(1)}, u32[]{:S(2)}, u32[]{:S(2)}) %collective-permute-start) | collective-permute-done | bytes 266272 | tf_op jit(solution)/shard_map/ppermute | solution.py:128
  80.4 2.6 %polish.1 = bf16[1024,512]{1,0:T(8,128)(2,1)S(1)} custom-call(bf16[1024,512]{1,0:T(8,128)(2,1)S(1)} %bitcast.3, bf16[520,256]{1,0:T(8,128)(2,1)S(1)} %gram.1.own, bf16[520,256]{1,0:T(8,128)(2,1)S(1)} %collective-permute-done.far), custom_call_target="tpu_custom_call" | custom-call | tf_op jit(solution)/shard_map/polish/pallas_call | solution.py:108
  83.0 32.2 %all_to_all.11 = bf16[16,64,512]{2,1,0:T(8,128)(2,1)S(1)} all-to-all(bf16[16,64,512]{2,1,0:T(8,128)(2,1)S(1)} %bitcast.4), channel_id=1, replica_groups=mesh['layer'=32,'y'=8,'z_hi'=2,'core'=2] {'y','core'}, dimensions={0} | all-to-all | bytes 2097152 | tf_op jit(solution)/shard_map/all_to_all | solution.py:120
  115.2 1.1 fusion.2
Async XLA Ops:
  39.2 41.2 %collective-permute-start = (bf16[520,256]{1,0:T(8,128)(2,1)S(1)}, bf16[520,256]{1,0:T(8,128)(2,1)S(1)}, u32[]{:S(2)}, u32[]{:S(2)}) collective-permute-start(bf16[520,256]{1,0:T(8,128)(2,1)S(1)} %gram.1.own), channel_id=1, source_target_pairs={{0,2},{2,0},{1,3},{3,1},{4,6},{6,4},{5,7},{7,5},{8,10},{10,8},{9,1... | collective-permute-start | bytes 798728 | tf_op jit(solution)/shard_map/ppermute | solution.py:128

commit v3 on v2

--- a/solution.py
+++ b/solution.py
@@ -77,10 +77,10 @@
     return (linear + COEF_C * product(current, current)).astype(jnp.bfloat16)
 
 
-def polish_kernel(rows, own, far, out, scaled):
-    half = own.shape[1]
+def polish_kernel(rows, halves, out, scaled):
+    half = halves.shape[2]
     row, column = positions(half)
-    packed = own[...].astype(jnp.float32) + far[...].astype(jnp.float32)
+    packed = halves[0].astype(jnp.float32) + halves[1].astype(jnp.float32)
     corner, both, diagonal = packed[:half], packed[half : 2 * half], packed[2 * half : 2 * half + 1]
     mirrored = both.T
     first = jnp.where(row < column, both, jnp.where(row == column, diagonal, mirrored))
@@ -103,17 +103,17 @@
     out[...] = (product(rows[...], combined) * (math.sqrt(D) * factor)).astype(jnp.bfloat16)
 
 
-def polish(rows, own, far):
+def polish(rows, halves):
     columns = rows.shape[1]
     return pl.pallas_call(
         polish_kernel,
         out_shape=jax.ShapeDtypeStruct(rows.shape, jnp.bfloat16),
-        in_specs=[IN_VMEM] * 3,
+        in_specs=[IN_VMEM] * 2,
         out_specs=IN_VMEM,
         scratch_shapes=[pltpu.VMEM((columns, columns), jnp.bfloat16)],
         compiler_params=pltpu.CompilerParams(vmem_limit_bytes=GRANT),
         name="polish",
-    )(rows, own, far)
+    )(rows, halves)
 
 
 def exchange(blocks):
@@ -125,8 +125,7 @@
     stacked = blend_all(gate_grad, gate_moment, down_grad, down_moment)
     owned_rows = exchange(stacked).reshape(-1, columns)
     own = gram(owned_rows)
-    far = lax.ppermute(own, "z_hi", [(0, 1), (1, 0)])
-    result = polish(owned_rows, own, far)
+    result = polish(owned_rows, lax.all_gather(own, "z_hi"))
     restored = exchange(result.reshape(2 * experts, row_count, columns))
     return restored[:experts], restored[experts:]
 

time: 117 us -> 115 us (0.983)
  blocking collectives: 68.2 us -> 108 us
  waiting for transfers between devices: 23 us -> 0 us
  starting transfers between devices: 18.2 us -> 0 us
    all_gather x0 -> x1, blocking collectives: none -> 40 us  [shards(): result = polish(owned_rows, lax.all_gather(own, 'z_hi'))]
    ppermute x1 -> x0, waiting for transfers between devices: 23 us -> none  [shards(): far = lax.ppermute(own, 'z_hi', [(0, 1), (1, 0)])]
    ppermute x1 -> x0, starting transfers between devices: 18.2 us -> none  [shards(): far = lax.ppermute(own, 'z_hi', [(0, 1), (1, 0)])]
  transfers between devices with their start and end apart: 1 -> 0, of which waited for: 1 -> 0; matrix products, arithmetic and copies ran while one was open for 0% -> 0% of each run, Pallas kernels for 0% -> 0%
where the time goes in v3:
time: 115 us
  blocking collectives  108 us (94%)
  Pallas kernels  3.21 us (3%)
  other arithmetic  1.96 us (2%)
    all_to_all x2, blocking collectives, exchange(): return lax.all_to_all(blocks, HALF, split_axis=0, concat_axis=0, tiled=True)  68.2 us
    all_gather x1, blocking collectives, shards(): result = polish(owned_rows, lax.all_gather(own, 'z_hi'))  40 us
    pallas_call x1, Pallas kernels, polish(): pl.pallas_call(polish_kernel, out_shape=jax.ShapeDtypeStruct(rows.shape,...  2.6 us

profile of v3, /device:TPU:71, one launch (start us, length us, event | category | flops | bytes accessed | tf_op | source)
XLA Modules:
  0.0 115.0 jit_solution(14324746285753839289)
XLA Ops:
  0.6 2.0 %fusion.1 = bf16[16,64,512]{2,1,0:T(8,128)(2,1)S(1)} fusion(bf16[8,64,512]{2,1,0:T(8,128)(2,1)} %param.6, bf16[8,64,512]{2,1,0:T(8,128)(2,1)} %param.4, bf16[8,64,512]{2,1,0:T(8,128)(2,1)} %param.7, bf16[8,64,512]{2,1,0:T(8,128)(2,1)} %param.5), kind=kLoop, calls=%fused_computation.3 | loop fusion | flops 4718592 | bytes 3145728 | tf_op jit(solution)/shard_map/convert_element_type | solution.py:27
  2.6 36.0 %all_to_all.10 = bf16[16,64,512]{2,1,0:T(8,128)(2,1)S(1)} all-to-all(bf16[16,64,512]{2,1,0:T(8,128)(2,1)S(1)} %fusion.1), channel_id=1, replica_groups=mesh['layer'=32,'y'=8,'z_hi'=2,'core'=2] {'y','core'}, dimensions={0} | all-to-all | bytes 2097152 | tf_op jit(solution)/shard_map/all_to_all | solution.py:120
  38.6 0.6 gram.1
  39.2 40.0 %all-gather = bf16[1040,256]{1,0:T(8,128)(2,1)S(1)} all-gather(bf16[520,256]{1,0:T(8,128)(2,1)S(1)} %gram.1), channel_id=2, replica_groups=mesh['layer'=32,'y'=8,'z_hi'=2,'core'=2] {'z_hi'}, dimensions={0}, use_global_device_ids=true | all-gather | bytes 798720 | tf_op jit(solution)/shard_map/all_gather | solution.py:128
  79.2 2.6 %polish.1 = bf16[1024,512]{1,0:T(8,128)(2,1)S(1)} custom-call(bf16[1024,512]{1,0:T(8,128)(2,1)S(1)} %bitcast.4, bf16[2,520,256]{2,1,0:T(8,128)(2,1)S(1)} %bitcast.6), custom_call_target="tpu_custom_call" | custom-call | tf_op jit(solution)/shard_map/polish/pallas_call | solution.py:108
  81.8 32.2 %all_to_all.11 = bf16[16,64,512]{2,1,0:T(8,128)(2,1)S(1)} all-to-all(bf16[16,64,512]{2,1,0:T(8,128)(2,1)S(1)} %bitcast.5), channel_id=1, replica_groups=mesh['layer'=32,'y'=8,'z_hi'=2,'core'=2] {'y','core'}, dimensions={0} | all-to-all | bytes 2097152 | tf_op jit(solution)/shard_map/all_to_all | solution.py:120
  114.0 1.1 fusion.2
